TPU v7x, 32 devices: a whole 2x2x4 slice. The times are simulated.
32 devices in a mesh: seq: 8 (over z, core), exp: 4 (over y, x).
Axes of the slice: x: 2, y: 2, z: 4, core: 2. Of those that a mesh axis runs over, the one named last changes fastest.
Arguments:
- queries: bfloat16 [768, 4096], P('seq', 'exp'), may hold values from -17 to 17
- keys: bfloat16 [768, 1024], P('seq', 'exp'), may hold values from -17 to 17
- values: bfloat16 [768, 1024], P('seq', 'exp'), may hold values from -6 to 6
- residual: bfloat16 [768, 4096], P('seq', 'exp'), may hold values from -48 to 48
- norm_gain: float32 [4096], P('exp'), may hold values from 0.1 to 1.9
- routes: int32 [768, 2], P('seq'), may hold values from 0 to 3, all different within a row; in each aligned block of 96 rows (0 to 95, 96 to 191, ...) at most 72 rows name the same one
- gates: float32 [768, 2], P('seq'), may hold values from 0.1 to 0.9
- w_gate: bfloat16 [4, 4096, 14336], P('exp', None, 'seq'), may hold values from -0.09375 to 0.09375
- w_up: bfloat16 [4, 4096, 14336], P('exp', None, 'seq'), may hold values from -0.09375 to 0.09375
- w_down: bfloat16 [4, 14336, 4096], P('exp', 'seq'), may hold values from -0.046875 to 0.046875
Outputs:
- attended: bfloat16 [768, 4096], P('seq', 'exp')
- layer_out: bfloat16 [768, 4096], P('seq', 'exp')
Inputs may be any that keep to these rules, and one draw needn't show every extreme that they name: `routes`: each row names 2 different experts. In the rows of one device no expert is named more than 72 times, a bound that some block reaches.
All inputs are finite; a program needn't handle non-finite values.
Results may differ from a plain program's by a relative error of at most 0.0075.
Values may be sent and summed in bfloat16 or wider, within the bound.
A program may use at most 128 MiB of HBM per device.

v0:
```python
import functools
import math

import jax
import jax.numpy as jnp
from jax import lax
from jax.experimental import pallas as pl
from jax.experimental.pallas import tpu as pltpu
from jax.sharding import PartitionSpec as P

D = 4096
QUERY_HEADS = 32
KEY_VALUE_HEADS = 8
HEAD_WIDTH = 128
TOP = 2
CORES = 2
LANES = 128
BF16 = jnp.bfloat16
F32 = jnp.float32


def place(chips, exp_count):
    seq, exp = lax.axis_index("seq"), lax.axis_index("exp")
    chip, core = seq // CORES, lax.rem(seq, CORES)
    far = lambda d: {"seq": lax.rem(chip + d, chips) * CORES + core, "exp": exp}
    partner = {"seq": chip * CORES + 1 - core, "exp": exp}
    side = lambda d: {"seq": seq, "exp": lax.rem(exp + d, exp_count)}
    return seq, exp, chip, core, far, partner, side


def greet(chips, exp_count, far, partner, side):
    barrier = pltpu.get_barrier_semaphore()
    targets = [partner]
    targets += [far(d) for d in range(1, chips)]
    targets += [side(d) for d in range(1, exp_count)]
    for target in targets:
        pl.semaphore_signal(barrier, inc=1, device_id=target, device_id_type=pl.DeviceIdType.MESH)
    pl.semaphore_wait(barrier, len(targets))


def remote(src, dst, send_sem, recv_sem, target):
    return pltpu.make_async_remote_copy(
        src_ref=src,
        dst_ref=dst,
        send_sem=send_sem,
        recv_sem=recv_sem,
        device_id=target,
        device_id_type=pl.DeviceIdType.MESH,
    )


def share_kernel(
    chips, exp_count, capacity, k_ref, v_ref, raw_ref, gain_ref,
    k_all, v_all, meta_all, gain_all,
    meta_ref, far_send, far_recv, fwd_send, fwd_recv, side_send, side_recv, local_sem,
):
    seq, exp, chip, core, far, partner, side = place(chips, exp_count)
    greet(chips, exp_count, far, partner, side)
    sent = []
    pairs = ((k_ref, k_all), (v_ref, v_all))
    for d in range(chips - 1, 0, -1):
        for i, (src, dst) in enumerate(pairs):
            c = remote(src, dst.at[seq], far_send.at[i, d], far_recv.at[i, d], far(d))
            c.start()
            sent.append(c)
    for d in range(1, exp_count):
        c = remote(gain_ref, gain_all.at[exp], side_send.at[d], side_recv.at[d], side(d))
        c.start()
        sent.append(c)
    for i, (src, dst) in enumerate(pairs):
        c = remote(src, dst.at[seq], fwd_send.at[i, 0], fwd_recv.at[i, 0], partner)
        c.start()
        sent.append(c)
    names = lax.broadcasted_iota(jnp.int32, raw_ref.shape, 0).astype(F32)
    one = [jnp.where(names == raw_ref[k : k + 1, :], 1.0, 0.0) for k in range(TOP)]
    lanes = (LANES, LANES)
    earlier = jnp.where(
        lax.broadcasted_iota(jnp.int32, lanes, 0) < lax.broadcasted_iota(jnp.int32, lanes, 1), 1.0, 0.0
    )
    before = jnp.dot(
        sum(one).astype(BF16), earlier.astype(BF16), preferred_element_type=F32
    )
    meta_ref[...] = raw_ref[...]
    for k in range(TOP):
        meta_ref[k : k + 1, :] = raw_ref[k : k + 1, :] * capacity + jnp.sum(
            one[k] * before, axis=0, keepdims=True
        )
    for d in range(chips - 1, 0, -1):
        c = remote(meta_ref, meta_all.at[chip], far_send.at[2, d], far_recv.at[2, d], far(d))
        c.start()
        sent.append(c)
    own = [
        pltpu.make_async_copy(src, dst, local_sem.at[i])
        for i, (src, dst) in enumerate(
            (
                (k_ref, k_all.at[seq]),
                (v_ref, v_all.at[seq]),
                (meta_ref, meta_all.at[chip]),
                (gain_ref, gain_all.at[exp]),
            )
        )
    ]
    for c in own:
        c.start()
    for d in range(1, chips):
        source = lax.rem(chip - d + chips, chips)
        block = source * CORES + core
        for i, (src, dst) in enumerate(pairs):
            remote(src, dst.at[block], far_send.at[i, d], far_recv.at[i, d], far(d)).wait_recv()
            c = remote(dst.at[block], dst.at[block], fwd_send.at[i, d], fwd_recv.at[i, d], partner)
            c.start()
            sent.append(c)
        remote(
            meta_ref, meta_all.at[source], far_send.at[2, d], far_recv.at[2, d], far(d)
        ).wait_recv()
    for d in range(1, exp_count):
        source = lax.rem(exp - d + exp_count, exp_count)
        remote(gain_ref, gain_all.at[source], side_send.at[d], side_recv.at[d], side(d)).wait_recv()
    for d in range(chips):
        block = lax.rem(chip - d + chips, chips) * CORES + 1 - core
        for i, (src, dst) in enumerate(pairs):
            remote(src, dst.at[block], fwd_send.at[i, d], fwd_recv.at[i, d], partner).wait_recv()
    for c in own:
        c.wait()
    for c in sent:
        c.wait_send()


def select_rows(dest, expert, member, capacity, iota):
    low = (expert * capacity).astype(F32)
    inside = (dest >= low) & (dest < low + capacity)
    return iota == jnp.where(inside, dest - low + (member * capacity).astype(F32), -1.0)


def gather_kernel(
    chips, exp_count, group, capacity, x_ref, meta_ref, gain_ref, gate_ref, up_ref, hidden_ref,
    out_ref, gate_mat, up_mat, tokens, outbox, inbox,
    far_send, far_recv, side_send, side_recv, pair_send, pair_recv, load_sem,
):
    seq, exp, chip, core, far, partner, side = place(chips, exp_count)
    blocks, depth, block = gate_mat.shape
    loads = []
    for i in range(blocks):
        for m, (src, dst) in enumerate(((gate_ref, gate_mat), (up_ref, up_mat))):
            c = pltpu.make_async_copy(
                src.at[:, i * block : (i + 1) * block], dst.at[i], load_sem.at[m, i]
            )
            c.start()
            loads.append(c)
    greet(chips, exp_count, far, partner, side)
    groups = chips // group
    tok_rows, width = x_ref.shape
    rows = group * capacity
    sent = []
    home, base = chip // group, lax.rem(chip, group)
    for slot in range(1, chips):
        turn, j = divmod(slot, group)
        target = lax.rem(home - turn + groups, groups) * group + lax.rem(base - j + group, group)
        c = remote(
            x_ref, tokens.at[slot], far_send.at[slot], far_recv.at[slot],
            {"seq": target * CORES + core, "exp": exp},
        )
        c.start()
        sent.append(c)
    tokens[0] = x_ref[...]
    iota = lax.broadcasted_iota(jnp.int32, (rows, tok_rows), 0).astype(F32)

    def dispatch(turn):
        which = lax.rem(home + turn, groups)
        members = []
        for j in range(group):
            place_of = lax.rem(base + j, group)
            slot = turn * group + j
            if slot:
                remote(
                    x_ref, tokens.at[slot], far_send.at[slot], far_recv.at[slot], partner
                ).wait_recv()
            members.append((which * group + place_of, place_of, slot))
        for step in range(exp_count):
            d = (step + 1) % exp_count
            expert = lax.rem(exp + d, exp_count)
            total = jnp.zeros((rows, width), F32)
            for source, member, slot in members:
                dest0 = meta_ref[source, 0:1, 0:tok_rows]
                dest1 = meta_ref[source, 1:2, 0:tok_rows]
                pick = select_rows(dest0, expert, member, capacity, iota) | select_rows(
                    dest1, expert, member, capacity, iota
                )
                total = total + jnp.dot(
                    jnp.where(pick, 1.0, 0.0).astype(BF16),
                    tokens[slot],
                    preferred_element_type=F32,
                )
            if d == 0:
                inbox[which, exp] = total.astype(BF16)
            else:
                outbox[turn, d - 1] = total.astype(BF16)
                c = remote(
                    outbox.at[turn, d - 1],
                    inbox.at[which, exp],
                    side_send.at[turn, d],
                    side_recv.at[turn, d],
                    side(d),
                )
                c.start()
                sent.append(c)

    def finish(turn):
        which = lax.rem(home + turn, groups)
        for d in range(1, exp_count):
            source = lax.rem(exp - d + exp_count, exp_count)
            remote(
                outbox.at[turn, d - 1],
                inbox.at[which, source],
                side_send.at[turn, d],
                side_recv.at[turn, d],
                side(d),
            ).wait_recv()
        step_rows = 16

        def norm(i, carry):
            at = pl.ds(pl.multiple_of(i * step_rows, step_rows), step_rows)
            square = jnp.zeros((step_rows, 1), F32)
            for e in range(exp_count):
                part = inbox[which, e, at, :].astype(F32)
                square = square + jnp.sum(part * part, axis=1, keepdims=True)
            scale = lax.rsqrt(square / (width * exp_count) + 1e-05)
            for e in range(exp_count):
                part = inbox[which, e, at, :].astype(F32)
                out_ref[which, core, at, e * width : (e + 1) * width] = (
                    part * scale * gain_ref[e, 0:1, :]
                ).astype(BF16)
            return carry

        lax.fori_loop(0, rows // step_rows, norm, 0)
        c = remote(
            out_ref.at[which, core],
            out_ref.at[which, core],
            pair_send.at[turn],
            pair_recv.at[turn],
            partner,
        )
        c.start()
        sent.append(c)

    for turn in range(groups):
        dispatch(turn)
    def expand(turn):
        which = lax.rem(home + turn, groups)
        remote(
            out_ref.at[which, core],
            out_ref.at[which, 1 - core],
            pair_send.at[turn],
            pair_recv.at[turn],
            partner,
        ).wait_recv()

        def one(i, carry):
            x = out_ref[which].reshape(CORES * rows, depth)
            gate = jnp.dot(x, gate_mat[i], preferred_element_type=F32)
            up = jnp.dot(x, up_mat[i], preferred_element_type=F32)
            hidden_ref[which, i] = (gate / (1.0 + jnp.exp(-gate)) * up).astype(BF16)
            return carry

        lax.fori_loop(0, blocks, one, 0)

    for c in loads:
        c.wait()
    for turn in range(groups):
        finish(turn)
        expand(turn)
    for c in sent:
        c.wait_send()


def return_kernel(
    chips, exp_count, group, capacity, hidden_ref, x_ref, meta_ref, down_ref, out_ref,
    down_mat, mine, peer, outbox, inbox, zout, zin,
    far_send, far_recv, side_send, side_recv, pair_send, pair_recv, load_sem,
):
    seq, exp, chip, core, far, partner, side = place(chips, exp_count)
    groups = chips // group
    tok_rows, width = x_ref.shape
    rows = group * capacity
    home = chip // group
    blocks, block = hidden_ref.shape[1], hidden_ref.shape[3]
    turns = [(step + 1) % exp_count for step in range(exp_count)]
    loads = {}
    for d in turns:
        columns = pl.ds(pl.multiple_of(lax.rem(exp + d, exp_count) * width, width), width)
        loads[d] = pltpu.make_async_copy(down_ref.at[:, columns], down_mat.at[d], load_sem.at[d])
        loads[d].start()
    greet(chips, exp_count, far, partner, side)
    order = list(range(1, groups)) + [0]
    sent = []

    def which_of(turn):
        return lax.rem(home - turn + groups, groups)

    def pair(turn, d):
        return remote(
            mine.at[turn, d, 1 - core],
            peer.at[turn, d],
            pair_send.at[turn, d],
            pair_recv.at[turn, d],
            partner,
        )

    def project(turn, d):
        which = which_of(turn)
        total = jnp.zeros((CORES * rows, width), F32)
        for i in range(blocks):
            total = total + jnp.dot(
                hidden_ref[which, i],
                down_mat[d, i * block : (i + 1) * block, :],
                preferred_element_type=F32,
            )
        mine[turn, d] = total.astype(BF16).reshape(CORES, rows, width)
        c = pair(turn, d)
        c.start()
        sent.append(c)

    def forward(turn, d):
        pair(turn, d).wait_recv()
        both = (mine[turn, d, core].astype(F32) + peer[turn, d].astype(F32)).astype(BF16)
        if d == 0:
            inbox[which_of(turn), exp] = both
        else:
            outbox[turn, d - 1] = both
            c = remote(
                outbox.at[turn, d - 1],
                inbox.at[which_of(turn), exp],
                side_send.at[turn, d],
                side_recv.at[turn, d],
                side(d),
            )
            c.start()
            sent.append(c)

    last = None
    for turn in order:
        for d in turns:
            if turn == order[0]:
                loads[d].wait()
            project(turn, d)
            if last is not None:
                forward(*last)
            last = (turn, d)
    forward(*last)
    iota = lax.broadcasted_iota(jnp.int32, (tok_rows, rows), 1).astype(F32)

    def mix(source, which, member):
        picked = [jnp.zeros((tok_rows, width), F32) for _ in range(TOP)]
        for e in range(exp_count):
            block = inbox[which, e]
            for k in range(TOP):
                dest = meta_ref[source, :, k : k + 1]
                low = float(e * capacity)
                inside = (dest >= low) & (dest < low + capacity)
                pick = iota == jnp.where(inside, dest - low + member.astype(F32) * capacity, -1.0)
                picked[k] = picked[k] + jnp.dot(
                    jnp.where(pick, 1.0, 0.0).astype(BF16), block, preferred_element_type=F32
                )
        total = jnp.zeros((tok_rows, width), F32)
        for k in range(TOP):
            total = total + picked[k] * meta_ref[source, :, TOP + k : TOP + k + 1]
        return total

    def arrive(turn):
        which = which_of(turn)
        for d in range(1, exp_count):
            source = lax.rem(exp - d + exp_count, exp_count)
            remote(
                outbox.at[turn, d - 1],
                inbox.at[which, source],
                side_send.at[turn, d],
                side_recv.at[turn, d],
                side(d),
            ).wait_recv()

    base = lax.rem(chip, group)
    total = None
    for turn in order:
        which = which_of(turn)
        arrive(turn)
        for j in range(group - 1, -1, -1):
            member = lax.rem(base + group - j, group)
            target = which * group + member
            part = mix(target, which, member)
            if turn == 0 and j == 0:
                total = part
            else:
                slot = turn * group + j
                zout[slot] = part.astype(BF16)
                c = remote(
                    zout.at[slot],
                    zin.at[slot],
                    far_send.at[slot],
                    far_recv.at[slot],
                    {"seq": target * CORES + core, "exp": exp},
                )
                c.start()
                sent.append(c)
    total = total + x_ref[...].astype(F32)
    for slot in range(1, chips):
        remote(
            zout.at[slot], zin.at[slot], far_send.at[slot], far_recv.at[slot], partner
        ).wait_recv()
        total = total + zin[slot].astype(F32)
    out_ref[...] = total.astype(BF16)
    for c in sent:
        c.wait_send()


def call(kernel, outs, scratch, collective_id, *args, streamed=()):
    vmem = pl.BlockSpec(memory_space=pltpu.VMEM)
    any_space = pl.BlockSpec(memory_space=pl.ANY)
    return pl.pallas_call(
        kernel,
        out_shape=outs,
        in_specs=[vmem] * len(args) + [any_space] * len(streamed),
        out_specs=jax.tree.map(lambda _: vmem, outs),
        scratch_shapes=scratch,
        compiler_params=pltpu.CompilerParams(
            collective_id=collective_id, has_side_effects=True, vmem_limit_bytes=56 * 2**20
        ),
    )(*args, *streamed)


def shards(queries, keys, values, residual, norm_gain, routes, gates, w_gate, w_up, w_down):
    tok_rows, local_width = queries.shape
    kv_width = keys.shape[1]
    local_heads = kv_width // HEAD_WIDTH
    group_width = QUERY_HEADS // KEY_VALUE_HEADS
    exp_count = lax.axis_size("exp")
    seq_count = lax.axis_size("seq")
    chips = seq_count // CORES
    dma = pltpu.SemaphoreType.DMA

    experts = exp_count * w_gate.shape[0]
    capacity = min(tok_rows, 3 * TOP * tok_rows // (2 * experts))
    group = 1
    while (group * capacity) % 16:
        group *= 2
    rows = group * capacity
    groups = chips // group

    raw = jnp.concatenate([routes.astype(F32), gates], axis=1).T
    raw = jnp.pad(
        raw, ((0, 8 - 2 * TOP), (0, LANES - tok_rows)), constant_values=-1.0
    )
    gain = norm_gain.reshape(1, local_width)

    k_all, v_all, meta_all, gain_all = call(
        functools.partial(share_kernel, chips, exp_count, capacity),
        (
            jax.ShapeDtypeStruct((seq_count, tok_rows, kv_width), BF16),
            jax.ShapeDtypeStruct((seq_count, tok_rows, kv_width), BF16),
            jax.ShapeDtypeStruct((chips, 8, LANES), F32),
            jax.ShapeDtypeStruct((exp_count, 1, local_width), F32),
        ),
        [
            pltpu.VMEM((8, LANES), F32),
            dma((3, chips)), dma((3, chips)), dma((2, chips)), dma((2, chips)),
            dma((exp_count,)), dma((exp_count,)), dma((4,)),
        ],
        1,
        keys, values, raw, gain,
    )

    score_scale = 1.0 / math.sqrt(HEAD_WIDTH)
    first_pos = lax.axis_index("seq") * tok_rows
    query_pos = first_pos + jnp.arange(tok_rows, dtype=jnp.int32)
    length = seq_count * tok_rows
    key_block = k_all.reshape(length, kv_width)
    value_block = v_all.reshape(length, kv_width)
    causal_mask = jnp.arange(length, dtype=jnp.int32)[None, :] <= query_pos[:, None]
    mask = jnp.concatenate([causal_mask] * group_width, axis=0)
    heads = []
    for h in range(local_heads):
        lanes = slice(h * HEAD_WIDTH, (h + 1) * HEAD_WIDTH)
        first = h * group_width * HEAD_WIDTH
        q = jnp.concatenate(
            [
                queries[:, first + i * HEAD_WIDTH : first + (i + 1) * HEAD_WIDTH]
                for i in range(group_width)
            ],
            axis=0,
        )
        scores = (
            lax.dot_general(
                q, key_block[:, lanes], (((1,), (1,)), ((), ())), preferred_element_type=F32
            )
            * score_scale
        )
        scores = jnp.where(mask, scores, -1e30)
        terms = jnp.where(mask, jnp.exp(scores - jnp.max(scores, axis=1, keepdims=True)), 0.0)
        weighted = jnp.dot(terms.astype(BF16), value_block[:, lanes], preferred_element_type=F32)
        out = weighted / jnp.sum(terms, axis=1, keepdims=True)
        heads += [out[i * tok_rows : (i + 1) * tok_rows] for i in range(group_width)]
    attn = jnp.concatenate(heads, axis=1)
    attended = (residual.astype(F32) + attn).astype(BF16)

    inner = w_gate.shape[2]
    block = 256 if inner % 256 == 0 else inner
    blocks = inner // block
    hidden = call(
        functools.partial(gather_kernel, chips, exp_count, group, capacity),
        jax.ShapeDtypeStruct((groups, blocks, CORES * rows, block), BF16),
        [
            pltpu.VMEM((groups, CORES, rows, exp_count * local_width), BF16),
            pltpu.VMEM((blocks, exp_count * local_width, block), BF16),
            pltpu.VMEM((blocks, exp_count * local_width, block), BF16),
            pltpu.VMEM((chips, tok_rows, local_width), BF16),
            pltpu.VMEM((groups, exp_count - 1, rows, local_width), BF16),
            pltpu.VMEM((groups, exp_count, rows, local_width), BF16),
            dma((chips,)), dma((chips,)),
            dma((groups, exp_count)), dma((groups, exp_count)),
            dma((groups,)), dma((groups,)),
            dma((2, blocks)),
        ],
        2,
        attended, meta_all, gain_all,
        streamed=(w_gate[0], w_up[0]),
    )
    meta_columns = jnp.swapaxes(meta_all, 1, 2)[:, :tok_rows, :]
    layer_out = call(
        functools.partial(return_kernel, chips, exp_count, group, capacity),
        jax.ShapeDtypeStruct((tok_rows, local_width), BF16),
        [
            pltpu.VMEM((exp_count, inner, local_width), BF16),
            pltpu.VMEM((groups, exp_count, CORES, rows, local_width), BF16),
            pltpu.VMEM((groups, exp_count, rows, local_width), BF16),
            pltpu.VMEM((groups, exp_count - 1, rows, local_width), BF16),
            pltpu.VMEM((groups, exp_count, rows, local_width), BF16),
            pltpu.VMEM((chips, tok_rows, local_width), BF16),
            pltpu.VMEM((chips, tok_rows, local_width), BF16),
            dma((chips,)), dma((chips,)),
            dma((groups, exp_count)), dma((groups, exp_count)),
            dma((groups, exp_count)), dma((groups, exp_count)),
            dma((exp_count,)),
        ],
        3,
        hidden, attended, meta_columns,
        streamed=(w_down[0],),
    )
    return (attended, layer_out)


def solution(mesh):
    in_specs = (
        P("seq", "exp"),
        P("seq", "exp"),
        P("seq", "exp"),
        P("seq", "exp"),
        P("exp"),
        P("seq", None),
        P("seq", None),
        P("exp", None, "seq"),
        P("exp", None, "seq"),
        P("exp", "seq", None),
    )
    out_specs = (P("seq", "exp"), P("seq", "exp"))
    return jax.shard_map(shards, mesh=mesh, in_specs=in_specs, out_specs=out_specs, check_vma=False)
```

profile of v0, /device:TPU:0, one launch (start us, length us, event | category | flops | bytes accessed | tf_op | source)
XLA Modules:
  0.0 133.7 jit_solution(76823907571761012)
XLA Ops:
  0.6 0.9 fusion.34
  1.5 0.7 convert_element_type.16
  2.2 0.7 maximum_bitcast_fusion
  2.9 0.6 pad.4.raw_ref
  3.5 18.8 %shard_map.113 = (bf16[8,96,256]{2,1,0:T(8,128)(2,1)}, bf16[8,96,256]{2,1,0:T(8,128)(2,1)}, f32[4,8,128]{2,1,0:T(8,128)}, f32[4,1,1024]{2,1,0:T(1,128)}) custom-call(bf16[96,256]{1,0:T(8,128)(2,1)} %k_ref.1, bf16[96,256]{1,0:T(8,128)(2,1)} %v_ref.1, f32[8,128]{1,0:T(8,128)} %pad.4.raw_ref, f32[1,1024]{1,0:T(1,128)} %bitcast.13), custom_call_target="tpu_custom_call" | custom-call | tf_op jit(solution)/shard_map/pallas_call | solution.py:418
  22.3 0.1 iota_compare_fusion
  22.4 0.0 copy-start.3
  22.5 1.4 %fusion.36 = (f32[384]{0:T(512)S(1)}, f32[384,768]{1,0:T(8,128)S(1)}) fusion(bf16[768,256]{1,0:T(8,128)(2,1)} %bitcast.16, bf16[96,128]{1,0:T(8,128)(2,1)S(1)} %get-tuple-element.18, bf16[96,128]{1,0:T(8,128)(2,1)S(1)} %get-tuple-element.19, bf16[96,128]{1,0:T(8,128)(2,1)S(1)} %get-tuple-element.13, bf16[96,128]{1,0:T(8,128)(2,1)S(1)} %get-tuple-element.12, ...), kind=kOutput, calls=%fused_computation.53 | convolution fusion | flops 77659776 | bytes 1549824 | tf_op jit(solution)/shard_map/dot_general | solution.py:491
  23.9 0.0 copy-done.3
  23.9 0.4 fusion.35
  24.3 0.0 copy-start.2
  24.3 0.8 fusion.4
  25.1 0.2 copy-done.2
  25.3 0.4 convolution_divide_fusion
  25.8 0.0 copy-start
  25.8 0.4 convolution_divide_fusion.1
  26.3 0.4 copy-done
  26.7 0.7 add_convert_fusion.x_ref
  27.4 0.0 copy-start.1
  27.4 58.6 %shard_map.114.hidden_ref = bf16[2,7,288,256]{3,2,1,0:T(8,128)(2,1)} custom-call(bf16[96,1024]{1,0:T(8,128)(2,1)} %add_convert_fusion.x_ref, f32[4,8,128]{2,1,0:T(8,128)} %get-tuple-element.8.meta_ref, f32[4,1,1024]{2,1,0:T(1,128)} %get-tuple-element.9.gain_ref, bf16[4096,1792]{1,0:T(8,128)(2,1)} %bitcast.9, bf16[4096,1792]{1,0:T(8,128)(2,1)} %bitcast.10), custom_call_target="tpu_custom_call" | custom-call | tf_op jit(solution)/shard_map/pallas_call | solution.py:418
  86.0 0.0 copy-done.1
  86.0 0.1 copy.12
  86.2 0.7 slice.96.meta_ref
  86.9 45.2 %shard_map.115 = bf16[96,1024]{1,0:T(8,128)(2,1)} custom-call(bf16[2,7,288,256]{3,2,1,0:T(8,128)(2,1)} %shard_map.114.hidden_ref, bf16[96,1024]{1,0:T(8,128)(2,1)} %add_convert_fusion.x_ref, f32[4,96,8]{2,1,0:T(8,128)} %slice.96.meta_ref, bf16[1792,4096]{1,0:T(8,128)(2,1)} %bitcast.11), custom_call_target="tpu_custom_call" | custom-call | tf_op jit(solution)/shard_map/pallas_call | solution.py:418
  132.1 1.6 %copy.27 = bf16[96,1024]{1,0:T(8,128)(2,1)} copy(bf16[96,1024]{1,0:T(8,128)(2,1)} %shard_map.115) | data formatting | bytes 393216
  (9 shorter events, 0.1 us)
Async XLA Ops:
  22.4 1.4 %copy-start.3 = (bf16[8,96,256]{2,1,0:T(8,128)(2,1)S(1)}, bf16[8,96,256]{2,1,0:T(8,128)(2,1)}, u32[]{:S(2)}) copy-start(bf16[8,96,256]{2,1,0:T(8,128)(2,1)} %get-tuple-element.6) | copy-start | bytes 1179652
  24.3 1.0 copy-start.2
  25.8 0.9 copy-start
  27.4 58.6 %copy-start.1 = (f32[4,8,128]{2,1,0:T(8,128)S(1)}, f32[4,8,128]{2,1,0:T(8,128)}, u32[]{:S(2)}) copy-start(f32[4,8,128]{2,1,0:T(8,128)} %get-tuple-element.8.meta_ref) | copy-start | bytes 49156
where the time goes:
time: 134 us
  Pallas kernels  123 us (92%)
  local copies, waits for them, and re-layouts  4.56 us (3%)
  other arithmetic  2.98 us (2%)
  matrix products  2.74 us (2%)
    pallas_call x3, Pallas kernels, call(): pl.pallas_call(kernel, out_shape=outs, in_specs=[vmem] * len(args) + [any...  123 us

commit v1 on v0

--- a/solution.py
+++ b/solution.py
@@ -1,5 +1,6 @@
 import functools
 import math
+import types
 
 import jax
 import jax.numpy as jnp
@@ -427,6 +428,650 @@
     )(*args, *streamed)
 
 
+def flip(index, step):
+    bit = 1
+    while bit <= step:
+        if step & bit:
+            index = index + bit - 2 * bit * lax.rem(index // bit, 2)
+        bit *= 2
+    return index
+
+
+RANKS = 4
+PLAN = (
+    "F0", "T1", "T2", "T3", "M0", "M1", "M2", "M3", "D0", "F1", "E3", "X0",
+    "Q0", "K0", "W0", "U003", "D1", "E2", "F2", "U037", "P0", "X1", "K1", "D2",
+    "W1", "U104", "F3", "B0", "U147", "X2", "P1", "D3", "K2", "W2", "R0", "U203",
+    "B1", "U235", "X3", "U257", "S0", "P2", "R1", "K3", "W3", "U303", "B2", "U335",
+    "S1", "U357", "R2", "P301", "P313", "B30", "P334", "S2", "B31", "R3", "S3",
+)
+
+
+def layer_kernel(names, chips, exp_count, capacity, *refs):
+    v = types.SimpleNamespace(**dict(zip(names, refs)))
+    seq, exp = lax.axis_index("seq"), lax.axis_index("exp")
+    chip, core = seq // CORES, lax.rem(seq, CORES)
+    other = 1 - core
+    tok_rows, width = v.queries.shape
+    head_lanes = HEAD_WIDTH
+    half = width // CORES
+    both_rows = CORES * tok_rows
+    rows = CORES * capacity
+    depth = exp_count * width
+    blocks = v.first_mat.shape[0]
+    block = v.first_mat.shape[2] // 2
+    inside = (chip > 0) & (chip < chips - 1)
+    source_of = [flip(chip, i) for i in range(chips)]
+    first = flip(exp, 1) * other + flip(exp, 2) * core
+    second = flip(exp, 2) * other + flip(exp, 1) * core
+    diag = flip(exp, 3)
+    j_first, j_second = 1 + core, 2 - core
+    at = lambda c, e=exp: {"seq": chip * CORES + c, "exp": e}
+    partner = at(other)
+    sent = []
+
+    def aligned(value, size, step):
+        return pl.ds(pl.multiple_of(value, step), size)
+
+    def send(src, dst, send_sem, recv_sem, target):
+        c = remote(src, dst, send_sem, recv_sem, target)
+        c.start()
+        sent.append(c)
+        return c
+
+    def arrived(dst, send_sem, recv_sem):
+        remote(dst, dst, send_sem, recv_sem, partner).wait_recv()
+
+    small = [
+        pltpu.make_async_copy(getattr(v, a), getattr(v, b), v.load_sem.at[i])
+        for i, (a, b) in enumerate(
+            (("keys", "k_in"), ("values", "v_in"), ("queries", "q_in"), ("residual", "r_in"))
+        )
+    ]
+    for c in small:
+        c.start()
+
+    raw = v.raw
+    raw[...] = jnp.full(raw.shape, -1.0, F32)
+    raw[0:TOP, 0:tok_rows] = v.routes[...].astype(F32)
+    raw[TOP : 2 * TOP, 0:tok_rows] = v.gates[...]
+    table = raw[...]
+    named = lax.broadcasted_iota(jnp.int32, table.shape, 0).astype(F32)
+    one = [jnp.where(named == table[k : k + 1, :], 1.0, 0.0) for k in range(TOP)]
+    lanes = (LANES, LANES)
+    earlier = jnp.where(
+        lax.broadcasted_iota(jnp.int32, lanes, 0) < lax.broadcasted_iota(jnp.int32, lanes, 1), 1.0, 0.0
+    )
+    before = jnp.dot(sum(one).astype(BF16), earlier.astype(BF16), preferred_element_type=F32)
+    meta = v.meta
+    meta[...] = table
+    for k in range(TOP):
+        meta[k : k + 1, :] = table[k : k + 1, :] * capacity + jnp.sum(
+            one[k] * before, axis=0, keepdims=True
+        )
+    v.k_all[...] = jnp.zeros(v.k_all.shape, BF16)
+    v.v_all[...] = jnp.zeros(v.v_all.shape, BF16)
+
+    barrier = pltpu.get_barrier_semaphore()
+    peers = [partner]
+    for d in range(1, chips):
+        for h in range(CORES):
+            peers.append({"seq": lax.rem(chip + d, chips) * CORES + h, "exp": exp})
+    for d in range(1, exp_count):
+        for h in range(CORES):
+            peers.append({"seq": chip * CORES + h, "exp": flip(exp, d)})
+    for target in peers:
+        pl.semaphore_signal(barrier, inc=1, device_id=target, device_id_type=pl.DeviceIdType.MESH)
+    pl.semaphore_wait(barrier, len(peers))
+
+    own_rows = aligned(seq * tok_rows, tok_rows, tok_rows)
+    small[0].wait()
+    small[1].wait()
+    pairs = (("k_in", "k_all"), ("v_in", "v_all"))
+    kv_send, kv_recv = v.kv_send, v.kv_recv
+    for d in range(chips - 1, 0, -1):
+
+        @pl.when(chip + d < chips)
+        def _():
+            for i, (a, b) in enumerate(pairs):
+                for h in range(CORES):
+                    remote(
+                        getattr(v, a).at[:, h * head_lanes : (h + 1) * head_lanes],
+                        getattr(v, b).at[own_rows, :],
+                        kv_send.at[i, d, h],
+                        kv_recv.at[i, d, core],
+                        {"seq": (chip + d) * CORES + h, "exp": exp},
+                    ).start()
+
+    for i, (a, b) in enumerate(pairs):
+        send(
+            getattr(v, a).at[:, aligned(other * head_lanes, head_lanes, head_lanes)],
+            getattr(v, b).at[own_rows, :],
+            kv_send.at[i, 0, 0],
+            kv_recv.at[i, 0, core],
+            partner,
+        )
+    mine_rows = aligned(core * tok_rows, tok_rows, tok_rows)
+    other_rows = aligned(other * tok_rows, tok_rows, tok_rows)
+    mine_lanes = aligned(core * half, half, half)
+    other_lanes = aligned(other * half, half, half)
+    small[2].wait()
+    small[3].wait()
+    for i, (a, b) in enumerate((("q_in", "q_half"), ("r_in", "r_half"))):
+        send(
+            getattr(v, a).at[:, other_lanes],
+            getattr(v, b).at[mine_rows, :],
+            v.pair_send.at[i],
+            v.pair_recv.at[i],
+            partner,
+        )
+    for d in range(chips):
+        for h in range(CORES):
+            if d:
+                target = {"seq": lax.rem(chip + d, chips) * CORES + h, "exp": exp}
+            elif h == 0:
+                target = partner
+            else:
+                continue
+            send(meta, v.meta_all.at[seq], v.meta_send.at[d, h], v.meta_recv.at[d, core], target)
+    loads = []
+    for i in range(blocks):
+        for m, a in enumerate(("w_gate", "w_up")):
+            loads.append(
+                pltpu.make_async_copy(
+                    getattr(v, a).at[:, i * block : (i + 1) * block],
+                    v.first_mat.at[i, :, m * block : (m + 1) * block],
+                    v.gate_sem.at[m, i],
+                )
+            )
+    for j in range(exp_count):
+        loads.append(
+            pltpu.make_async_copy(
+                v.w_down.at[:, j * width : (j + 1) * width], v.down_mat.at[j], v.down_sem.at[j]
+            )
+        )
+    for c in loads:
+        c.start()
+    v.meta_all[seq] = meta[...]
+    for a, b in pairs:
+        getattr(v, b)[own_rows, :] = getattr(v, a)[:, aligned(core * head_lanes, head_lanes, head_lanes)]
+    for a, b in (("q_in", "q_half"), ("r_in", "r_half")):
+        getattr(v, b)[mine_rows, :] = getattr(v, a)[:, mine_lanes]
+
+    for i, b in enumerate(("q_half", "r_half")):
+        arrived(getattr(v, b).at[other_rows, :], v.pair_send.at[i], v.pair_recv.at[i])
+    for i, (a, b) in enumerate(pairs):
+        there = aligned((chip * CORES + other) * tok_rows, tok_rows, tok_rows)
+        arrived(getattr(v, b).at[there, :], kv_send.at[i, 0, 0], kv_recv.at[i, 0, other])
+    for d in range(1, chips):
+
+        @pl.when(chip - d >= 0)
+        def _():
+            for i, (a, b) in enumerate(pairs):
+                for h in range(CORES):
+                    there = aligned(((chip - d) * CORES + h) * tok_rows, tok_rows, tok_rows)
+                    arrived(getattr(v, b).at[there, :], kv_send.at[i, d, h], kv_recv.at[i, d, h])
+
+    length = v.k_all.shape[0]
+    score_scale = 1.0 / math.sqrt(HEAD_WIDTH)
+    shape = (both_rows, length)
+    reach = lax.broadcasted_iota(jnp.int32, shape, 0) + chip * both_rows
+    mask = lax.broadcasted_iota(jnp.int32, shape, 1) <= reach
+    att = v.att
+    square = jnp.zeros((both_rows, 1), F32)
+    for i in range(half // HEAD_WIDTH):
+        part = slice(i * HEAD_WIDTH, (i + 1) * HEAD_WIDTH)
+        scores = (
+            lax.dot_general(
+                v.q_half[:, part], v.k_all[...], (((1,), (1,)), ((), ())),
+                preferred_element_type=F32,
+            )
+            * score_scale
+        )
+        scores = jnp.where(mask, scores, -1e30)
+        terms = jnp.where(mask, jnp.exp(scores - jnp.max(scores, axis=1, keepdims=True)), 0.0)
+        weighted = jnp.dot(terms.astype(BF16), v.v_all[...], preferred_element_type=F32)
+        value = weighted / jnp.sum(terms, axis=1, keepdims=True)
+        value = (v.r_half[:, part].astype(F32) + value).astype(BF16)
+        att[:, part] = value
+        value = value.astype(F32)
+        square = square + jnp.sum(value * value, axis=1, keepdims=True)
+    block_eye = lax.broadcasted_iota(jnp.int32, (tok_rows, LANES), 0) == lax.broadcasted_iota(
+        jnp.int32, (tok_rows, LANES), 1
+    )
+    squares, scales = v.squares, v.scales
+    tokens, near, x_full, peer = v.tokens, v.near, v.x_full, v.peer
+    tokens[chip] = (att[...].astype(F32) * v.gain[:, mine_lanes]).astype(BF16)
+
+    def ship(source, wait):
+        for way, test, to in ((0, (source <= chip) & (chip + 1 < chips), 1), (1, (source >= chip) & (chip > 0), -1)):
+
+            @pl.when(test)
+            def _():
+                c = remote(
+                    tokens.at[source], tokens.at[source],
+                    v.far_send.at[source, way], v.far_recv.at[source],
+                    {"seq": (chip + to) * CORES + core, "exp": exp},
+                )
+                if wait:
+                    c.wait_send()
+                else:
+                    c.start()
+
+    def landed(source):
+        arrived(tokens.at[source], v.far_send.at[source, 0], v.far_recv.at[source])
+
+    ship(chip, False)
+
+    def deliver(which, ref):
+        send(
+            ref.at[other_rows, :], v.theirs.at[which],
+            v.pair_send.at[2 + which], v.pair_recv.at[2 + which], partner,
+        )
+        c = pltpu.make_async_copy(
+            ref.at[mine_rows, :], v.ours.at[which], v.store_sem.at[which]
+        )
+        c.start()
+        stores.append(c)
+
+    stores = []
+
+    def spread():
+        for b in range(CORES):
+            squares[core, exp, b : b + 1, :] = jnp.sum(
+                jnp.where(block_eye, square[b * tok_rows : (b + 1) * tok_rows], 0.0), axis=0, keepdims=True
+            )
+        for d in range(exp_count):
+            for h in range(CORES):
+                if d:
+                    target = at(h, flip(exp, d))
+                elif h == 0:
+                    target = partner
+                else:
+                    continue
+                send(
+                    squares.at[core, exp], squares.at[core, exp],
+                    v.square_send.at[d, h], v.square_recv.at[d, core], target,
+                )
+        deliver(0, att)
+        for d in range(chips):
+            for h in range(CORES):
+                source = lax.rem(chip - d + chips, chips)
+                if d:
+                    arrived(
+                        v.meta_all.at[source * CORES + h], v.meta_send.at[d, h], v.meta_recv.at[d, h]
+                    )
+                elif h == 0:
+                    arrived(
+                        v.meta_all.at[chip * CORES + other],
+                        v.meta_send.at[0, 0], v.meta_recv.at[0, other],
+                    )
+
+    def stage_q(i):
+        arrived(squares.at[other, exp], v.square_send.at[0, 0], v.square_recv.at[0, other])
+        for d in range(1, exp_count):
+            for h in range(CORES):
+                arrived(squares.at[h, flip(exp, d)], v.square_send.at[d, h], v.square_recv.at[d, h])
+        total = jnp.zeros(squares.shape[2:], F32)
+        for e in range(exp_count):
+            for h in range(CORES):
+                total = total + squares[h, e]
+        scales[chip] = lax.rsqrt(total / depth + 1e-05)
+        for d in range(1, chips):
+            send(
+                scales.at[chip], scales.at[chip], v.scale_send.at[d], v.scale_recv.at[d],
+                {"seq": lax.rem(chip + d, chips) * CORES + core, "exp": exp},
+            )
+
+    on_first, on_second = at(core, first), at(core, second)
+    pair_of = {}
+
+    def lane_of(slice_at, c):
+        return aligned(slice_at * width + c * half, half, half)
+
+    def give(turn, piece, slice_at):
+        place = x_full.at[turn, :, lane_of(slice_at, core)]
+        pair_of[turn, piece] = send(
+            place, place, v.give_send.at[turn, piece], v.give_recv.at[turn, piece], partner
+        )
+
+    def tables(turn):
+        iota = lax.broadcasted_iota(jnp.int32, (capacity, tok_rows), 0).astype(F32)
+        hits, named = [], []
+        for b in range(CORES):
+            names_of = v.meta_all[source_of[turn] * CORES + b]
+            dest = [names_of[k : k + 1, 0:tok_rows] for k in range(TOP)]
+            hits.append([[iota == dest[k] - low[x] for k in range(TOP)] for x in range(2)])
+            named.append(names_of)
+        return hits, named
+
+    low = [(e * capacity).astype(F32) for e in (exp, second)]
+
+    def gathered(turn, value):
+        out = [
+            jnp.dot(
+                v.picks[turn, b], value[b * tok_rows : (b + 1) * tok_rows, :], preferred_element_type=F32
+            )
+            for b in range(CORES)
+        ]
+        return [
+            jnp.concatenate([o[x * capacity : (x + 1) * capacity] for o in out], axis=0).astype(BF16)
+            for x in range(2)
+        ]
+
+    def stage_f(turn):
+        source = source_of[turn]
+        if turn == 1:
+            landed(source)
+            ship(source, False)
+        elif turn:
+
+            @pl.when(jnp.logical_not(inside))
+            def _():
+                landed(source)
+
+        send(tokens.at[source], near.at[turn], v.near_send.at[turn], v.near_recv.at[turn], on_first)
+        if turn == 0:
+            spread()
+            stage_t(turn)
+        mine, away = gathered(turn, tokens[source])
+        v.outbox[turn, 0] = away
+        x_full[turn, :, lane_of(exp, core)] = mine
+        push(turn, 0, exp)
+        give(turn, 0, exp)
+
+    def stage_t(turn):
+        hits, _ = tables(turn)
+        for b in range(CORES):
+            v.picks[turn, b] = jnp.concatenate(
+                [jnp.where(hits[b][x][0] | hits[b][x][1], 1.0, 0.0) for x in range(2)], axis=0
+            ).astype(BF16)
+
+    def stage_e(turn):
+        @pl.when(inside)
+        def _():
+            landed(source_of[turn])
+            ship(source_of[turn], False)
+
+    def stage_d(turn):
+        arrived(near.at[turn], v.near_send.at[turn], v.near_recv.at[turn])
+        mine, away = gathered(turn, near[turn])
+        v.outbox[turn, 1] = away
+        x_full[turn, :, lane_of(first, core)] = mine
+        push(turn, 1, first)
+        give(turn, 1, first)
+
+    def stage_k(turn):
+        source = source_of[turn]
+        if turn:
+            for d in range(1, chips):
+
+                @pl.when(lax.rem(chip - source + chips, chips) == d)
+                def _():
+                    arrived(scales.at[source], v.scale_send.at[d], v.scale_recv.at[d])
+
+        hits, named = tables(turn)
+        weights, norms = [], []
+        for b in range(CORES):
+            mine = hits[b][0]
+            gate = [named[b][TOP + k : TOP + k + 1, 0:tok_rows] for k in range(TOP)]
+            weights.append(
+                sum(jnp.sum(jnp.where(mine[k], gate[k], 0.0), axis=1, keepdims=True) for k in range(TOP))
+            )
+            norm = scales[source, b : b + 1, 0:tok_rows]
+            norms.append(
+                sum(jnp.sum(jnp.where(mine[k], norm, 0.0), axis=1, keepdims=True) for k in range(TOP))
+            )
+        v.row_gate[turn] = jnp.broadcast_to(jnp.concatenate(weights, axis=0), (rows, LANES))
+        v.row_norm[turn] = jnp.broadcast_to(jnp.concatenate(norms, axis=0), (rows, LANES))
+
+    def stage_m(turn):
+        place_of = lax.broadcasted_iota(jnp.int32, (tok_rows, rows), 1).astype(F32)
+        for b in range(CORES):
+            names_of = v.meta_all[source_of[turn] * CORES + b]
+            columns = [
+                jnp.sum(jnp.where(block_eye, names_of[k : k + 1, :], 0.0), axis=1, keepdims=True)
+                for k in range(TOP)
+            ]
+            for x in range(2):
+                mark = None
+                for k in range(TOP):
+                    column = columns[k] - low[x]
+                    column = jnp.where(
+                        (column >= 0.0) & (column < capacity), column + float(b * capacity), -1.0
+                    )
+                    hit = place_of == column
+                    mark = hit if mark is None else mark | hit
+                v.mixer[turn, x, b * tok_rows : (b + 1) * tok_rows, :] = jnp.where(mark, 1.0, 0.0).astype(BF16)
+
+    def push(turn, piece, slice_at):
+        send(
+            v.outbox.at[turn, piece],
+            x_full.at[turn, :, lane_of(slice_at, core)],
+            v.push_send.at[turn, piece],
+            v.push_recv.at[turn, piece],
+            on_second,
+        )
+
+    def stage_x(turn):
+        for piece, slice_at in ((0, second), (1, diag)):
+            arrived(
+                x_full.at[turn, :, lane_of(slice_at, core)],
+                v.push_send.at[turn, piece],
+                v.push_recv.at[turn, piece],
+            )
+            give(turn, 2 + piece, slice_at)
+
+    def stage_w(turn):
+        for piece, slice_at in enumerate((exp, second, first, diag)):
+            arrived(
+                x_full.at[turn, :, lane_of(slice_at, other)],
+                v.give_send.at[turn, piece],
+                v.give_recv.at[turn, piece],
+            )
+
+    def stage_u(turn, start, stop):
+        start, stop = (blocks * start // 7, blocks * stop // 7)
+        if turn == 0:
+            for c in loads[2 * start : 2 * stop]:
+                c.wait()
+
+        def one(i, carry):
+            out = jnp.dot(x_full[turn], v.first_mat[i], preferred_element_type=F32)
+            norm = v.row_norm[turn, :, 0:1]
+            gate = out[:, :block] * norm
+            up = out[:, block:] * norm
+            v.hidden[turn, :, aligned(i * block, block, block)] = (
+                gate / (1.0 + jnp.exp(-gate)) * up
+            ).astype(BF16)
+            return carry
+
+        lax.fori_loop(start, stop, one, 0)
+
+    down_ready = []
+
+    def stage_p(turn, start=0, stop=RANKS):
+        if not down_ready:
+            for c in loads[2 * blocks :]:
+                c.wait()
+            down_ready.append(True)
+        for piece in range(4):
+            if start:
+                break
+            c = pair_of[turn, piece]
+            c.wait_send()
+            sent[:] = [o for o in sent if o is not c]
+
+        def one(step, carry):
+            j = exp_count - 1 - step
+            slice_at = exp + lax.rem(j, 2) * (1 - 2 * lax.rem(exp, 2)) + (j // 2) * (2 - 4 * (exp // 2))
+            out = jnp.dot(v.hidden[turn], v.down_mat[slice_at], preferred_element_type=F32)
+            x_full[turn, :, aligned(slice_at * width, width, width)] = out.astype(BF16)
+            swap(turn, j, slice_at).start()
+            return carry
+
+        lax.fori_loop(start, stop, one, 0)
+        for step in range(start, stop):
+            j = exp_count - 1 - step
+            sent.append(swap(turn, j, flip(exp, j)))
+
+    def swap(turn, j, slice_at):
+        return remote(
+            x_full.at[turn, :, lane_of(slice_at, other)],
+            peer.at[turn, j],
+            v.peer_send.at[turn, j],
+            v.peer_recv.at[turn, j],
+            partner,
+        )
+
+    def stage_b(turn, part=None):
+        weight = v.row_gate[turn, :, 0:1]
+        last = exp_count - 1
+        slices = {None: range(last, -1, -1), 0: [last], 1: range(last - 1, -1, -1)}[part]
+        for j in slices:
+            arrived(peer.at[turn, j], v.peer_send.at[turn, j], v.peer_recv.at[turn, j])
+            total = x_full[turn, :, lane_of(flip(exp, j), core)].astype(F32) + peer[turn, j].astype(F32)
+            peer[turn, j] = (total * weight).astype(BF16)
+        pieces = ((1, last), (0, j_second))
+        for piece, j in pieces if part is None else [pieces[part]]:
+            send(
+                peer.at[turn, j], v.back.at[turn, piece],
+                v.back_send.at[turn, piece], v.back_recv.at[turn, piece], on_second,
+            )
+
+    def mixed(turn, j, piece):
+        arrived(v.back.at[turn, piece], v.back_send.at[turn, piece], v.back_recv.at[turn, piece])
+        return jnp.dot(v.mixer[turn, 0], peer[turn, j], preferred_element_type=F32) + jnp.dot(
+            v.mixer[turn, 1], v.back[turn, piece], preferred_element_type=F32
+        )
+
+    def stage_r(turn):
+        v.near_out[turn] = mixed(turn, j_first, 1).astype(BF16)
+        send(
+            v.near_out.at[turn], v.near_in.at[turn],
+            v.home_send.at[turn], v.home_recv.at[turn], on_first,
+        )
+
+    def stage_s(turn):
+        total = mixed(turn, 0, 0)
+        arrived(v.near_in.at[turn], v.home_send.at[turn], v.home_recv.at[turn])
+        total = total + v.near_in[turn].astype(F32)
+        if turn == 0:
+            v.total[...] = total + att[...].astype(F32)
+        else:
+            v.far_out[turn - 1] = total.astype(BF16)
+            send(
+                v.far_out.at[turn - 1], v.far_in.at[chip],
+                v.last_send.at[turn], v.last_recv.at[chip],
+                {"seq": source_of[turn] * CORES + core, "exp": exp},
+            )
+
+    stages = {
+        "F": stage_f, "D": stage_d, "X": stage_x, "W": stage_w, "U": stage_u, "E": stage_e,
+        "P": stage_p, "B": stage_b, "R": stage_r, "S": stage_s, "Q": stage_q, "K": stage_k, "M": stage_m, "T": stage_t,
+    }
+    for step in PLAN:
+        stages[step[0]](*map(int, step[1:]))
+    total = v.total[...]
+    for turn in range(1, chips):
+        source = source_of[turn]
+        arrived(v.far_in.at[source], v.last_send.at[turn], v.last_recv.at[source])
+        total = total + v.far_in[source].astype(F32)
+    v.q_half[...] = total.astype(BF16)
+    deliver(1, v.q_half)
+    for i in range(2):
+        stores[i].wait()
+        arrived(v.theirs.at[i], v.pair_send.at[2 + i], v.pair_recv.at[2 + i])
+    for turn in range(chips):
+        ship(source_of[turn], True)
+    for c in sent:
+        c.wait_send()
+    for d in range(chips - 1, 0, -1):
+
+        @pl.when(chip + d < chips)
+        def _():
+            for i, (a, b) in enumerate(pairs):
+                for h in range(CORES):
+                    remote(
+                        getattr(v, a).at[:, h * head_lanes : (h + 1) * head_lanes],
+                        getattr(v, b).at[own_rows, :],
+                        kv_send.at[i, d, h],
+                        kv_recv.at[i, d, core],
+                        {"seq": (chip + d) * CORES + h, "exp": exp},
+                    ).wait_send()
+
+
+def fused(queries, keys, values, residual, norm_gain, routes, gates, w_gate, w_up, w_down, capacity):
+    tok_rows, width = queries.shape
+    kv_width = keys.shape[1]
+    exp_count, seq_count = lax.axis_size("exp"), lax.axis_size("seq")
+    chips = seq_count // CORES
+    depth, inner = w_gate.shape[1:]
+    half, both_rows, rows = width // CORES, CORES * tok_rows, CORES * capacity
+    block = 2 * LANES if inner % (2 * LANES) == 0 else inner
+    blocks = inner // block
+    dma = pltpu.SemaphoreType.DMA
+    bf = lambda *shape: pltpu.VMEM(shape, BF16)
+    f32 = lambda *shape: pltpu.VMEM(shape, F32)
+    inputs = dict(
+        gain=norm_gain.reshape(1, width), routes=routes.T, gates=gates.T,
+        queries=queries, keys=keys, values=values, residual=residual,
+        w_gate=w_gate[0], w_up=w_up[0], w_down=w_down[0],
+    )
+    scratch = dict(
+        k_in=bf(tok_rows, kv_width), v_in=bf(tok_rows, kv_width),
+        q_in=bf(tok_rows, width), r_in=bf(tok_rows, width),
+        q_half=bf(both_rows, half), r_half=bf(both_rows, half),
+        k_all=bf(seq_count * tok_rows, HEAD_WIDTH), v_all=bf(seq_count * tok_rows, HEAD_WIDTH),
+        raw=f32(8, LANES), meta=f32(8, LANES), meta_all=f32(seq_count, 8, LANES),
+        squares=f32(CORES, exp_count, 8, LANES), scales=f32(chips, 8, LANES),
+        att=bf(both_rows, half), total=f32(both_rows, half),
+        tokens=bf(chips, both_rows, half), near=bf(chips, both_rows, half),
+        outbox=bf(chips, 2, rows, half), x_full=bf(chips, rows, depth),
+        peer=bf(chips, exp_count, rows, half), back=bf(chips, 2, rows, half),
+        near_out=bf(chips, both_rows, half), near_in=bf(chips, both_rows, half),
+        far_out=bf(chips - 1, both_rows, half), far_in=bf(chips, both_rows, half),
+        row_gate=f32(chips, rows, LANES), row_norm=f32(chips, rows, LANES),
+        picks=bf(chips, CORES, rows, tok_rows), mixer=bf(chips, 2, both_rows, rows),
+        hidden=bf(chips, rows, inner),
+        first_mat=bf(blocks, depth, 2 * block),
+        down_mat=bf(exp_count, inner, width),
+        load_sem=dma((4,)), store_sem=dma((2,)), gate_sem=dma((2, blocks)), down_sem=dma((exp_count,)),
+        kv_send=dma((2, chips, CORES)), kv_recv=dma((2, chips, CORES)),
+        pair_send=dma((4,)), pair_recv=dma((4,)),
+        meta_send=dma((chips, CORES)), meta_recv=dma((chips, CORES)),
+        square_send=dma((exp_count, CORES)), square_recv=dma((exp_count, CORES)),
+        far_send=dma((chips, 2)), far_recv=dma((chips,)),
+        scale_send=dma((chips,)), scale_recv=dma((chips,)),
+        near_send=dma((chips,)), near_recv=dma((chips,)),
+        push_send=dma((chips, 2)), push_recv=dma((chips, 2)),
+        give_send=dma((chips, 4)), give_recv=dma((chips, 4)),
+        peer_send=dma((chips, exp_count)), peer_recv=dma((chips, exp_count)),
+        back_send=dma((chips, 2)), back_recv=dma((chips, 2)),
+        home_send=dma((chips,)), home_recv=dma((chips,)),
+        last_send=dma((chips,)), last_recv=dma((chips,)),
+    )
+    vmem = pl.BlockSpec(memory_space=pltpu.VMEM)
+    any_space = pl.BlockSpec(memory_space=pl.ANY)
+    out = jax.ShapeDtypeStruct((2, tok_rows, half), BF16)
+    names = list(inputs) + ["ours", "theirs"] + list(scratch)
+    ours, theirs = pl.pallas_call(
+        functools.partial(layer_kernel, names, chips, exp_count, capacity),
+        out_shape=(out, out),
+        in_specs=[vmem] * 3 + [any_space] * (len(inputs) - 3),
+        out_specs=(any_space, any_space),
+        scratch_shapes=list(scratch.values()),
+        compiler_params=pltpu.CompilerParams(
+            collective_id=1, has_side_effects=True, vmem_limit_bytes=67043328
+        ),
+    )(*inputs.values())
+    left_is_ours = lax.rem(lax.axis_index("seq"), CORES) == 0
+    both = jnp.concatenate(
+        [jnp.where(left_is_ours, ours, theirs), jnp.where(left_is_ours, theirs, ours)], axis=2
+    )
+    return both[0], both[1]
+
+
 def shards(queries, keys, values, residual, norm_gain, routes, gates, w_gate, w_up, w_down):
     tok_rows, local_width = queries.shape
     kv_width = keys.shape[1]
@@ -444,6 +1089,10 @@
         group *= 2
     rows = group * capacity
     groups = chips // group
+    if exp_count == 4 and chips == RANKS and local_heads == CORES and capacity % 8 == 0:
+        return fused(
+            queries, keys, values, residual, norm_gain, routes, gates, w_gate, w_up, w_down, capacity
+        )
 
     raw = jnp.concatenate([routes.astype(F32), gates], axis=1).T
     raw = jnp.pad(

time: 134 us -> 97 us (0.72)
  the two profiles are of different devices: /device:TPU:0 before, /device:TPU:9 now
where the time goes in v1:
time: 97 us; the launch traced here: 96.8 us
  Pallas kernels  94.3 us (97%)
  other arithmetic  1.84 us (2%)
    pallas_call x1, Pallas kernels, fused(): pl.pallas_call(functools.partial(layer_kernel, names, chips, exp_count, c...  94.3 us

profile of v1, /device:TPU:9, one launch (start us, length us, event | category | flops | bytes accessed | tf_op | source)
XLA Modules:
  0.0 96.8 jit_solution(14256081885582930790)
XLA Ops:
  0.6 94.3 %shard_map.113 = (bf16[2,96,512]{2,1,0:T(8,128)(2,1)}, bf16[2,96,512]{2,1,0:T(8,128)(2,1)}) custom-call(f32[1,1024]{1,0:T(1,128)} %bitcast.13, s32[2,96]{1,0:T(2,128)} %bitcast.14, f32[2,96]{1,0:T(2,128)} %bitcast.15, bf16[96,1024]{1,0:T(8,128)(2,1)} %refs_3_.1, bf16[96,256]{1,0:T(8,128)(2,1)} %refs_4_.1, bf16[96,256]{1,0:T(8,128)(2,1)} %refs_5_.1, ...), custom_call_target="tpu_custom_call" | custom-call | tf_op jit(solution)/shard_map/pallas_call | solution.py:1058
  94.9 1.1 %broadcast_select_fusion = (bf16[2,96,512]{2,1,0:T(8,128)(2,1)S(1)}, bf16[2,96,512]{2,1,0:T(8,128)(2,1)S(1)}) fusion(bf16[2,96,512]{2,1,0:T(8,128)(2,1)} %get-tuple-element.5, bf16[2,96,512]{2,1,0:T(8,128)(2,1)} %get-tuple-element.4, pred[]{:T(512)S(6)} %eq.3), kind=kLoop, calls=%fused_computation.6 | loop fusion | flops 196608 | bytes 786433 | tf_op jit(solution)/shard_map/jit(_where)/select_n | solution.py:1070
  96.0 0.8 fusion.2
